TPU v7x, 256 devices: a whole 4x4x8 slice. The times are simulated.
256 devices in a mesh: dp: 32 (over y, z), rows: 8 (over x, core).
Axes of the slice: x: 4, y: 4, z: 8, core: 2. Of those that a mesh axis runs over, the one named last changes fastest.
Arguments:
- latent: float32 [32, 128, 32, 128], P('dp', 'rows'), may hold values from -12 to 12
- bits1: int32 [32, 16, 32, 16], P('dp', 'rows'), may hold values from -1 to 1, as said below
- bits2: int32 [32, 32, 32, 32], P('dp', 'rows'), may hold values from -1 to 1, as said below
- bits3: int32 [32, 64, 32, 64], P('dp', 'rows'), may hold values from -1 to 1, as said below
- bits4: int32 [32, 128, 32, 128], P('dp', 'rows'), may hold values from -1 to 1, as said below
- w_in: bfloat16 [3, 3, 32, 256], replicated, may hold values from -0.375 to 0.375
- w_mid: bfloat16 [3, 3, 256, 256], replicated, may hold values from -0.125 to 0.125
- w_out: bfloat16 [3, 3, 32, 256], replicated, may hold values from -0.125 to 0.125
Outputs:
- recon: float32 [32, 128, 32, 128], P('dp', 'rows')
- usage_entropy: float32 [4, 8], replicated
- sample_entropy: float32 [4], replicated
Inputs may be any that keep to these rules, and one draw needn't show every extreme that they name: `bits1`: each entry is -1 or +1. `bits2`: each entry is -1 or +1. `bits3`: each entry is -1 or +1. `bits4`: each entry is -1 or +1.
All inputs are finite; a program needn't handle non-finite values.
Results may differ from a plain program's by a relative error of at most 0.0021.
Values may be sent and summed in bfloat16 or wider, within the bound.
A program may use at most 64 MiB of HBM per device.

v0:
```python
import functools

import jax
import jax.numpy as jnp
from jax import lax
from jax.experimental import pallas as pl
from jax.experimental.pallas import tpu as pltpu
from jax.sharding import PartitionSpec as P

MESH = pl.DeviceIdType.MESH
F32 = jnp.float32
BF16 = jnp.bfloat16
FACTORS = (8, 4, 2, 1)
HALO = (1, 2, 2, 3)
SHARPNESS = 2.0
EPSILON = 1e-6
ROWS = 16
CH = 32
HID = 256
W = 128
PAIRS = ROWS // 2


def lanes(shape):
    return lax.broadcasted_iota(jnp.int32, shape, len(shape) - 1)


def subs(shape):
    return lax.broadcasted_iota(jnp.int32, shape, len(shape) - 2)


def side_masks(dtype):
    lane = lanes((1, W))
    low = jnp.where(lane == 0, 0.0, 1.0).astype(dtype)
    high = jnp.where(lane == W - 1, 0.0, 1.0).astype(dtype)
    return low, high


def from_left(x, low):
    return pltpu.roll(x, 1, 1) * low


def from_right(x, high):
    return pltpu.roll(x, W - 1, 1) * high


def gelu(x):
    inner = x * (0.7978845608028654 + (0.7978845608028654 * 0.044715) * (x * x))
    half = 0.5 * x
    return half + half * jnp.tanh(inner)


def block_mean(x, factor):
    lane = lanes(x.shape)
    step = 1
    while step < factor:
        below = pltpu.roll(x, step, 1)
        above = pltpu.roll(x, W - step, 1)
        x = x + jnp.where((lane & step) == 0, above, below)
        step *= 2
    return x * (1.0 / (factor * factor))


def column_table(side, factor):
    shape = (side, W)
    target = lanes(shape)
    row = subs(shape)
    shift = (2 * factor).bit_length() - 1
    numerator = 2 * target + 1 - factor
    lower = lax.shift_right_arithmetic(numerator, jnp.full(shape, shift, jnp.int32))
    fraction = (numerator - 2 * factor * lower).astype(F32) * (1.0 / (2.0 * factor))
    low_at = jnp.clip(lower, 0, side - 1)
    high_at = jnp.clip(lower + 1, 0, side - 1)
    table = jnp.where(row == low_at, 1.0 - fraction, 0.0) + jnp.where(
        row == high_at, fraction, 0.0
    )
    return table.astype(BF16)


def body(
    ny,
    nz,
    nr,
    lat,
    b1,
    b2,
    b3,
    b4,
    w_in,
    w_mid,
    w_out,
    recon,
    uent,
    sent,
    w1,
    w2,
    w3,
    xs,
    fs,
    gs,
    ub,
    cs,
    ps,
    qs,
    h1,
    h2,
    h3,
    h4,
    mags,
    tot,
    part_r,
    part_y,
    part_z,
    halo_ss,
    halo_rs,
    mag_ss,
    mag_rs,
    pr_ss,
    pr_rs,
    py_ss,
    py_rs,
    pz_ss,
    pz_rs,
):
    bits = (b1, b2, b3, b4)
    halos = (h1, h2, h3, h4)
    me = lax.axis_index("rows")
    dp = lax.axis_index("dp")
    my_y = dp // nz
    my_z = dp % nz
    is_first = me == 0
    is_last = me == nr - 1

    def row_peer(d):
        return lax.rem(me + d, nr)

    def y_peer(d):
        return lax.rem(my_y + d, ny)

    def z_peer(d):
        return lax.rem(my_z + d, nz)

    barrier = pltpu.get_barrier_semaphore()
    for d in range(1, nr):
        pl.semaphore_signal(barrier, inc=1, device_id={"rows": row_peer(d)}, device_id_type=MESH)
    for d in range(1, ny):
        pl.semaphore_signal(
            barrier, inc=1, device_id={"dp": y_peer(d) * nz + my_z}, device_id_type=MESH
        )
    for d in range(1, nz):
        pl.semaphore_signal(
            barrier, inc=1, device_id={"dp": my_y * nz + z_peer(d)}, device_id_type=MESH
        )

    def halo_copy(level, side):
        count = ROWS // FACTORS[level]
        keep = HALO[level]
        if side == 0:
            src = bits[level].at[0, pl.ds(count - keep, keep)]
            target = me + 1
        else:
            src = bits[level].at[0, pl.ds(0, keep)]
            target = me - 1
        return pltpu.make_async_remote_copy(
            src_ref=src,
            dst_ref=halos[level].at[side],
            send_sem=halo_ss.at[level, side],
            recv_sem=halo_rs.at[level, side],
            device_id={"rows": target},
            device_id_type=MESH,
        )

    def halo_send(level):
        @pl.when(jnp.logical_not(is_last))
        def _():
            halo_copy(level, 0).start()

        @pl.when(jnp.logical_not(is_first))
        def _():
            halo_copy(level, 1).start()

    def halo_wait(level):
        @pl.when(jnp.logical_not(is_first))
        def _():
            halo_copy(level, 0).wait_recv()

        @pl.when(jnp.logical_not(is_last))
        def _():
            halo_copy(level, 1).wait_recv()

    def halo_drain(level):
        @pl.when(jnp.logical_not(is_last))
        def _():
            halo_copy(level, 0).wait_send()

        @pl.when(jnp.logical_not(is_first))
        def _():
            halo_copy(level, 1).wait_send()

    def mag_copy(level, d, slot):
        return pltpu.make_async_remote_copy(
            src_ref=mags.at[level, slot],
            dst_ref=mags.at[level, slot],
            send_sem=mag_ss.at[level, d],
            recv_sem=mag_rs.at[level, slot],
            device_id={"rows": row_peer(d)},
            device_id_type=MESH,
        )

    def stage_copy(buf, ss, rs, d, slot, target):
        return pltpu.make_async_remote_copy(
            src_ref=buf.at[slot],
            dst_ref=buf.at[slot],
            send_sem=ss.at[d],
            recv_sem=rs.at[slot],
            device_id=target,
            device_id_type=MESH,
        )

    def r_copy(d, slot):
        return stage_copy(part_r, pr_ss, pr_rs, d, slot, {"rows": row_peer(d)})

    def y_copy(d, slot):
        return stage_copy(part_y, py_ss, py_rs, d, slot, {"dp": y_peer(d) * nz + my_z})

    def z_copy(d, slot):
        return stage_copy(part_z, pz_ss, pz_rs, d, slot, {"dp": my_y * nz + z_peer(d)})

    def residual_row(level, row):
        if level == 0:
            return lat[0, row]
        return lat[0, row] - recon[0, row]

    def coarse_stage(level):
        factor = FACTORS[level]
        count = ROWS // factor
        total = jnp.zeros((CH, W), F32)
        for i in range(count):
            acc = residual_row(level, i * factor)
            for j in range(1, factor):
                acc = acc + residual_row(level, i * factor + j)
            acc = block_mean(acc, factor)
            cs[i] = acc
            total = total + jnp.abs(acc)
        summed = jnp.sum(total, axis=1, keepdims=True)
        shape = (CH, W)
        row = jnp.sum(
            jnp.where(lanes(shape) == subs(shape), jnp.broadcast_to(summed, shape), 0.0),
            axis=0,
            keepdims=True,
        )
        mags[level, me] = row

    def mag_send(level):
        for d in range(1, nr):
            mag_copy(level, d, me).start()

    def mag_wait(level):
        for d in range(1, nr):
            mag_copy(level, d, row_peer(d)).wait_recv()
        factor = FACTORS[level]
        side = W // factor
        row = mags[level, 0]
        for j in range(1, nr):
            row = row + mags[level, j]
        shape = (CH, W)
        spread = jnp.where(lanes(shape) == subs(shape), jnp.broadcast_to(row, shape), 0.0)
        return jnp.sum(spread, axis=1, keepdims=True) * (1.0 / (factor * side * side))

    def stats_stage(level):
        factor = FACTORS[level]
        count = ROWS // factor
        entropy = jnp.zeros((8, W), F32)
        for i in range(count):
            logits = (SHARPNESS * factor) * cs[i]
            size = jnp.abs(logits)
            small = jnp.exp(-size)
            inverse = 1.0 / (1.0 + small)
            rest = small * inverse
            each = jnp.log1p(small) + size * rest
            entropy = entropy + (each[0:8] + each[8:16]) + (each[16:24] + each[24:32])
            positive = logits >= 0.0
            ps[i] = jnp.where(positive, inverse, rest)
            qs[i] = jnp.where(positive, rest, inverse)
        sums = [jnp.zeros((8, W), F32) for _ in range(16)]
        for i in range(count):
            one = [ps[i, pl.ds(k, 8, stride=4)] for k in range(4)]
            zero = [qs[i, pl.ds(k, 8, stride=4)] for k in range(4)]
            front = [x * y for x in (zero[0], one[0]) for y in (zero[1], one[1])]
            back = [x * y for x in (zero[2], one[2]) for y in (zero[3], one[3])]
            for j in range(16):
                sums[j] = sums[j] + front[j // 4] * back[j % 4]
        lane = lanes((8, W))
        tile = jnp.zeros((8, W), F32) if level == 0 else tot[...]
        for j in range(16):
            tile = tile + jnp.where(
                lane == level * 16 + j, jnp.sum(sums[j], axis=1, keepdims=True), 0.0
            )
        tile = tile + jnp.where(lane == 64 + level, jnp.sum(entropy, axis=1, keepdims=True), 0.0)
        tot[...] = tile

    def spread_stage(level):
        factor = FACTORS[level]
        count = ROWS // factor
        keep = HALO[level]
        side = W // factor
        ref = bits[level]
        top = halos[level][0]
        bottom = halos[level][1]
        own_top = jnp.broadcast_to(ref[0, 0][None], (keep, CH, side))
        own_bottom = jnp.broadcast_to(ref[0, count - 1][None], (keep, CH, side))
        top = jnp.where(is_first, own_top, top)
        bottom = jnp.where(is_last, own_bottom, bottom)
        if factor == 1:
            for u in range(3):
                ub[u] = top[u].astype(F32)
                ub[ROWS + 3 + u] = bottom[u].astype(F32)
            for u in range(ROWS):
                ub[u + 3] = ref[0, u].astype(F32)
            return
        stack = jnp.concatenate([top, ref[0], bottom], axis=0).astype(F32).astype(BF16)
        stack = stack.reshape((count + 2 * keep) * CH, side)
        wide = jnp.dot(stack, column_table(side, factor), preferred_element_type=F32)
        wide = wide.reshape(count + 2 * keep, CH, W)
        for u in range(ROWS + 6):
            numerator = 2 * (u - 3) + 1 - factor
            lower = numerator // (2 * factor)
            fraction = (numerator - 2 * factor * lower) / (2.0 * factor)
            at = lower + keep
            ub[u] = (1.0 - fraction) * wide[at] + fraction * wide[at + 1]

    def scale_stage(level, magnitude):
        low, high = side_masks(BF16)
        wide = jnp.broadcast_to(magnitude, (CH, W))
        top = jnp.where(is_first, 0.0, 1.0)
        bottom = jnp.where(is_last, 0.0, 1.0)
        for u in range(ROWS + 6):
            up = ub[u] * wide
            if u < 3:
                up = up * top
            elif u >= ROWS + 3:
                up = up * bottom
            elif level == 0:
                recon[0, u - 3] = up
            else:
                recon[0, u - 3] = recon[0, u - 3] + up
            half = up.astype(BF16)
            xs[u, 0:CH] = from_left(half, low)
            xs[u, CH : 2 * CH] = half
            xs[u, 2 * CH : 3 * CH] = from_right(half, high)

    def window(ref, row):
        a = ref[row : row + 3]
        b = ref[row + 1 : row + 4]
        depth = 3 * a.shape[1]
        return jnp.concatenate([a.reshape(depth, W), b.reshape(depth, W)], axis=1)

    def first_pair(p):
        low, high = side_masks(BF16)
        z = gelu(jnp.dot(w1[...], window(xs, 2 * p), preferred_element_type=F32))
        if p == 0:
            z = z * jnp.where(is_first, 0.0, 1.0)
        if p == PAIRS + 1:
            z = z * jnp.where(is_last, 0.0, 1.0)
        z = z.astype(BF16)
        for h in range(2):
            x = z[:, h * W : (h + 1) * W]
            fs[2 * p + h, 0:HID] = from_left(x, low)
            fs[2 * p + h, HID : 2 * HID] = x
            fs[2 * p + h, 2 * HID : 3 * HID] = from_right(x, high)

    def second_pair(p):
        z = gelu(jnp.dot(w2[...], window(fs, 2 * p), preferred_element_type=F32))
        for h in range(2):
            x = z[:, h * W : (h + 1) * W]
            if p == 0 and h == 0:
                x = x * jnp.where(is_first, 0.0, 1.0)
            if p == PAIRS and h == 1:
                x = x * jnp.where(is_last, 0.0, 1.0)
            gs[2 * p + h] = x.astype(BF16)

    def third_pair(p):
        low, high = side_masks(F32)
        z = jnp.dot(w3[...], window(gs, 2 * p), preferred_element_type=F32)
        for h in range(2):
            x = z[:, h * W : (h + 1) * W]
            recon[0, 2 * p + h] = recon[0, 2 * p + h] + (
                x[CH : 2 * CH] + from_left(x[0:CH], low) + from_right(x[2 * CH : 3 * CH], high)
            )

    flat_in = w_in[...].reshape(9 * CH, HID)
    w1[...] = flat_in.T
    for tap in range(9):
        w2[:, tap * HID : (tap + 1) * HID] = w_mid[tap // 3, tap % 3].T
    for dr in range(3):
        for dc in range(3):
            w3[dc * CH : (dc + 1) * CH, dr * HID : (dr + 1) * HID] = w_out[dr, dc]

    coarse_stage(0)
    pl.semaphore_wait(barrier, (nr - 1) + (ny - 1) + (nz - 1))
    mag_send(0)
    halo_send(0)
    for level in range(1, 4):
        halo_send(level)

    def one_level(level, _):
        for k in range(4):

            @pl.when(level == k)
            def _(k=k):
                if k > 0:
                    coarse_stage(k)
                    mag_send(k)
                stats_stage(k)
                halo_wait(k)
                spread_stage(k)
                if k == 3:
                    part_r[me] = tot[...]
                    for d in range(1, nr):
                        r_copy(d, me).start()
                scale_stage(k, mag_wait(k))

        for p in range(PAIRS + 4):
            if p < PAIRS + 2:
                first_pair(p)
            if 2 <= p < PAIRS + 3:
                second_pair(p - 2)
            if p >= 4:
                third_pair(p - 4)
            if p == 4:

                @pl.when(level == 3)
                def _():
                    for d in range(1, nr):
                        r_copy(d, row_peer(d)).wait_recv()
                    tile = part_r[0]
                    for j in range(1, nr):
                        tile = tile + part_r[j]
                    part_y[my_y] = tile
                    for d in range(1, ny):
                        y_copy(d, my_y).start()

            if p == 7:

                @pl.when(level == 3)
                def _():
                    for d in range(1, ny):
                        y_copy(d, y_peer(d)).wait_recv()
                    tile = part_y[0]
                    for j in range(1, ny):
                        tile = tile + part_y[j]
                    part_z[my_z] = tile
                    for d in range(1, nz):
                        z_copy(d, my_z).start()

        return 0

    lax.fori_loop(0, 4, one_level, 0)

    for d in range(1, nz):
        z_copy(d, z_peer(d)).wait_recv()
    tile = part_z[0]
    for j in range(1, nz):
        tile = tile + part_z[j]
    lane = lanes((8, W))
    images = ny * nz
    group = lane // 16
    scale = jnp.zeros((8, W), F32)
    for level in range(4):
        side = W // FACTORS[level]
        scale = jnp.where(
            group == level, 1.0 / (images * side * side * FACTORS[level]), scale
        )
    usage = tile * scale
    terms = -(usage * jnp.log(usage + EPSILON))
    square = (8, W)
    for level in range(4):
        mine = jnp.sum(jnp.where(group == level, terms, 0.0), axis=1, keepdims=True)
        row = jnp.sum(
            jnp.where(lanes(square) == subs(square), jnp.broadcast_to(mine, square), 0.0),
            axis=0,
            keepdims=True,
        )
        uent[level : level + 1, :] = row[:, 0:8]
    entropies = jnp.sum(tile, axis=0, keepdims=True)
    shifted = pltpu.roll(entropies, W - 64, 1)
    lane1 = lanes((1, W))
    scale1 = jnp.zeros((1, W), F32)
    for level in range(4):
        side = W // FACTORS[level]
        scale1 = jnp.where(
            lane1 == level, 1.0 / (images * side * side * FACTORS[level] * CH), scale1
        )
    sent[...] = (shifted * scale1)[:, 0:4]

    for level in range(4):
        halo_drain(level)
        for d in range(1, nr):
            mag_copy(level, d, me).wait_send()
    for d in range(1, nr):
        r_copy(d, me).wait_send()
    for d in range(1, ny):
        y_copy(d, my_y).wait_send()
    for d in range(1, nz):
        z_copy(d, my_z).wait_send()


def solution(mesh):
    nd = mesh.shape["dp"]
    nr = mesh.shape["rows"]
    ny = 4 if nd % 4 == 0 and nd >= 16 else 1
    nz = nd // ny

    vmem = pl.BlockSpec(memory_space=pltpu.VMEM)
    dma = pltpu.SemaphoreType.DMA

    def on_device(*args):
        recon, uent, sent = pl.pallas_call(
            functools.partial(body, ny, nz, nr),
            out_shape=(
                jax.ShapeDtypeStruct((1, ROWS, CH, W), F32),
                jax.ShapeDtypeStruct((4, 8), F32),
                jax.ShapeDtypeStruct((1, 4), F32),
            ),
            in_specs=[vmem] * 8,
            out_specs=(vmem, vmem, vmem),
            scratch_shapes=[
                pltpu.VMEM((HID, 9 * CH), BF16),
                pltpu.VMEM((HID, 9 * HID), BF16),
                pltpu.VMEM((3 * CH, 3 * HID), BF16),
                pltpu.VMEM((ROWS + 6, 3 * CH, W), BF16),
                pltpu.VMEM((ROWS + 4, 3 * HID, W), BF16),
                pltpu.VMEM((ROWS + 2, HID, W), BF16),
                pltpu.VMEM((ROWS + 6, CH, W), F32),
                pltpu.VMEM((ROWS, CH, W), F32),
                pltpu.VMEM((ROWS, CH, W), F32),
                pltpu.VMEM((ROWS, CH, W), F32),
                pltpu.VMEM((2, HALO[0], CH, 16), jnp.int32),
                pltpu.VMEM((2, HALO[1], CH, 32), jnp.int32),
                pltpu.VMEM((2, HALO[2], CH, 64), jnp.int32),
                pltpu.VMEM((2, HALO[3], CH, 128), jnp.int32),
                pltpu.VMEM((4, nr, 1, W), F32),
                pltpu.VMEM((8, W), F32),
                pltpu.VMEM((nr, 8, W), F32),
                pltpu.VMEM((ny, 8, W), F32),
                pltpu.VMEM((nz, 8, W), F32),
                dma((4, 2)),
                dma((4, 2)),
                dma((4, nr)),
                dma((4, nr)),
                dma((nr,)),
                dma((nr,)),
                dma((ny,)),
                dma((ny,)),
                dma((nz,)),
                dma((nz,)),
            ],
            compiler_params=pltpu.CompilerParams(
                collective_id=0, has_side_effects=True, vmem_limit_bytes=60 * 1024 * 1024
            ),
        )(*args)
        return recon, uent, sent.reshape(4)

    split = P("dp", "rows", None, None)
    return jax.shard_map(
        on_device,
        mesh=mesh,
        in_specs=(split,) * 5 + (P(),) * 3,
        out_specs=(split, P(), P()),
        check_vma=False,
    )
```

profile of v0, /device:TPU:1, one launch (start us, length us, event | category | flops | bytes accessed | tf_op | source)
XLA Modules:
  0.0 60.7 jit_solution(17253543876172493198)
XLA Ops:
  0.6 1.4 %copy.11.b1 = s32[1,2,32,16]{3,2,1,0:T(8,128)} copy(s32[1,2,32,16]{2,3,1,0:T(8,128)} %param.9) | data formatting | bytes 8192 | tf_op args[1]
  2.0 54.7 %shard_map.103 = (f32[1,16,32,128]{3,2,1,0:T(8,128)}, f32[4,8]{1,0:T(4,128)}, f32[1,4]{1,0:T(1,128)}) custom-call(f32[1,16,32,128]{3,2,1,0:T(8,128)} %lat.1, s32[1,2,32,16]{3,2,1,0:T(8,128)} %copy.11.b1, s32[1,4,32,32]{3,2,1,0:T(8,128)} %b2.1, s32[1,8,32,64]{3,2,1,0:T(8,128)} %b3.1, s32[1,16,32,128]{3,2,1,0:T(8,128)} %b4.1, bf16[3,3,32,256]{3,2,1,0:T(8,128)(2,1)} %w_in.1, ...), custom_call_target="tpu_custom_call" | custom-call | tf_op jit(solution)/shard_map/pallas_call | solution.py:518
  56.7 1.7 %copy.15 = f32[1,16,32,128]{3,2,1,0:T(8,128)} copy(f32[1,16,32,128]{3,2,1,0:T(8,128)} %get-tuple-element.12) | data formatting | bytes 524288
  58.4 1.2 %copy.16 = f32[4,8]{1,0:T(4,128)} copy(f32[4,8]{1,0:T(4,128)} %get-tuple-element.13) | data formatting | bytes 256
  59.7 1.1 %copy.17 = f32[4]{0:T(128)} copy(f32[4]{0:T(128)} %bitcast.1) | data formatting | bytes 32
where the time goes:
time: 61 us; the launch traced here: 60.7 us
  Pallas kernels  54.7 us (90%)
  local copies, waits for them, and re-layouts  5.41 us (9%)
  between operations  0.64 us (1%)
    pallas_call x1, Pallas kernels, on_device(): pl.pallas_call(functools.partial(body, ny, nz, nr), out_shape=(jax.ShapeD...  54.7 us
    unnamed x4, local copies, waits for them, and re-layouts  5.41 us

commit v1 on v0

--- a/solution.py
+++ b/solution.py
@@ -14,11 +14,13 @@
 HALO = (1, 2, 2, 3)
 SHARPNESS = 2.0
 EPSILON = 1e-6
+VMEM_LIMIT = 66000000
 ROWS = 16
 CH = 32
 HID = 256
 W = 128
 PAIRS = ROWS // 2
+SPLIT = (0, PAIRS)
 
 
 def lanes(shape):
@@ -81,6 +83,16 @@
     ny,
     nz,
     nr,
+    lat_in,
+    b1_in,
+    b2_in,
+    b3_in,
+    b4_in,
+    w_in_in,
+    w_mid_in,
+    w_out_in,
+    recon,
+    final,
     lat,
     b1,
     b2,
@@ -89,9 +101,6 @@
     w_in,
     w_mid,
     w_out,
-    recon,
-    uent,
-    sent,
     w1,
     w2,
     w3,
@@ -107,20 +116,20 @@
     h3,
     h4,
     mags,
-    tot,
+    mg,
+    st,
     part_r,
-    part_y,
-    part_z,
+    part_d,
+    in_sem,
     halo_ss,
     halo_rs,
     mag_ss,
     mag_rs,
     pr_ss,
     pr_rs,
-    py_ss,
-    py_rs,
-    pz_ss,
-    pz_rs,
+    pd_ss,
+    pd_rs,
+    near,
 ):
     bits = (b1, b2, b3, b4)
     halos = (h1, h2, h3, h4)
@@ -134,23 +143,36 @@
     def row_peer(d):
         return lax.rem(me + d, nr)
 
-    def y_peer(d):
-        return lax.rem(my_y + d, ny)
-
-    def z_peer(d):
-        return lax.rem(my_z + d, nz)
+    def dp_peer(d):
+        return lax.rem(my_y + d // nz, ny) * nz + lax.rem(my_z + d % nz, nz)
+
+    steps = [] if nz == 1 else [1, nz - 1]
+    steps = steps + ([] if ny == 1 else [nz, (ny - 1) * nz])
 
     barrier = pltpu.get_barrier_semaphore()
     for d in range(1, nr):
         pl.semaphore_signal(barrier, inc=1, device_id={"rows": row_peer(d)}, device_id_type=MESH)
-    for d in range(1, ny):
-        pl.semaphore_signal(
-            barrier, inc=1, device_id={"dp": y_peer(d) * nz + my_z}, device_id_type=MESH
-        )
-    for d in range(1, nz):
-        pl.semaphore_signal(
-            barrier, inc=1, device_id={"dp": my_y * nz + z_peer(d)}, device_id_type=MESH
-        )
+    for d in steps:
+        pl.semaphore_signal(barrier, inc=1, device_id={"dp": dp_peer(d)}, device_id_type=MESH)
+
+    def near_send():
+        for n, d in enumerate(steps):
+            pl.semaphore_signal(
+                near.at[n], inc=1, device_id={"dp": dp_peer(d)}, device_id_type=MESH
+            )
+
+    def near_wait():
+        for n in range(len(steps)):
+            pl.semaphore_wait(near.at[n], 1)
+
+    hbm = (lat_in, b1_in, w_in_in, w_out_in, w_mid_in, b2_in, b3_in, b4_in)
+    local = (lat, b1, w_in, w_out, w_mid, b2, b3, b4)
+
+    def fetch(n):
+        return pltpu.make_async_copy(hbm[n], local[n], in_sem.at[n])
+
+    for n in range(8):
+        fetch(n).start()
 
     def halo_copy(level, side):
         count = ROWS // FACTORS[level]
@@ -220,11 +242,8 @@
     def r_copy(d, slot):
         return stage_copy(part_r, pr_ss, pr_rs, d, slot, {"rows": row_peer(d)})
 
-    def y_copy(d, slot):
-        return stage_copy(part_y, py_ss, py_rs, d, slot, {"dp": y_peer(d) * nz + my_z})
-
-    def z_copy(d, slot):
-        return stage_copy(part_z, pz_ss, pz_rs, d, slot, {"dp": my_y * nz + z_peer(d)})
+    def d_copy(d, slot):
+        return stage_copy(part_d, pd_ss, pd_rs, d, slot, {"dp": dp_peer(d)})
 
     def residual_row(level, row):
         if level == 0:
@@ -291,13 +310,17 @@
             for j in range(16):
                 sums[j] = sums[j] + front[j // 4] * back[j % 4]
         lane = lanes((8, W))
-        tile = jnp.zeros((8, W), F32) if level == 0 else tot[...]
+        place = lane - 16 * subs((8, W))
+        tile = jnp.zeros((8, W), F32)
         for j in range(16):
-            tile = tile + jnp.where(
-                lane == level * 16 + j, jnp.sum(sums[j], axis=1, keepdims=True), 0.0
-            )
-        tile = tile + jnp.where(lane == 64 + level, jnp.sum(entropy, axis=1, keepdims=True), 0.0)
-        tot[...] = tile
+            tile = tile + jnp.where(place == j, jnp.sum(sums[j], axis=1, keepdims=True), 0.0)
+        st[level] = jnp.sum(tile, axis=0, keepdims=True)
+        flat = jnp.sum(
+            jnp.where(lane == level, jnp.sum(entropy, axis=1, keepdims=True), 0.0),
+            axis=0,
+            keepdims=True,
+        )
+        st[4] = flat if level == 0 else st[4] + flat
 
     def spread_stage(level):
         factor = FACTORS[level]
@@ -307,8 +330,9 @@
         ref = bits[level]
         top = halos[level][0]
         bottom = halos[level][1]
-        own_top = jnp.broadcast_to(ref[0, 0][None], (keep, CH, side))
-        own_bottom = jnp.broadcast_to(ref[0, count - 1][None], (keep, CH, side))
+        plane = (side, CH) if level == 0 else (CH, side)
+        own_top = jnp.broadcast_to(ref[0, 0][None], (keep, *plane))
+        own_bottom = jnp.broadcast_to(ref[0, count - 1][None], (keep, *plane))
         top = jnp.where(is_first, own_top, top)
         bottom = jnp.where(is_last, own_bottom, bottom)
         if factor == 1:
@@ -319,9 +343,18 @@
                 ub[u + 3] = ref[0, u].astype(F32)
             return
         stack = jnp.concatenate([top, ref[0], bottom], axis=0).astype(F32).astype(BF16)
-        stack = stack.reshape((count + 2 * keep) * CH, side)
-        wide = jnp.dot(stack, column_table(side, factor), preferred_element_type=F32)
-        wide = wide.reshape(count + 2 * keep, CH, W)
+        table = column_table(side, factor)
+        if level == 0:
+            wide = [
+                lax.dot_general(
+                    stack[n], table, (((0,), (0,)), ((), ())), preferred_element_type=F32
+                )
+                for n in range(count + 2 * keep)
+            ]
+        else:
+            stack = stack.reshape((count + 2 * keep) * CH, side)
+            wide = jnp.dot(stack, table, preferred_element_type=F32)
+            wide = wide.reshape(count + 2 * keep, CH, W)
         for u in range(ROWS + 6):
             numerator = 2 * (u - 3) + 1 - factor
             lower = numerator // (2 * factor)
@@ -329,25 +362,19 @@
             at = lower + keep
             ub[u] = (1.0 - fraction) * wide[at] + fraction * wide[at + 1]
 
-    def scale_stage(level, magnitude):
+    def scale_row(u):
         low, high = side_masks(BF16)
-        wide = jnp.broadcast_to(magnitude, (CH, W))
-        top = jnp.where(is_first, 0.0, 1.0)
-        bottom = jnp.where(is_last, 0.0, 1.0)
-        for u in range(ROWS + 6):
-            up = ub[u] * wide
-            if u < 3:
-                up = up * top
-            elif u >= ROWS + 3:
-                up = up * bottom
-            elif level == 0:
-                recon[0, u - 3] = up
-            else:
-                recon[0, u - 3] = recon[0, u - 3] + up
-            half = up.astype(BF16)
-            xs[u, 0:CH] = from_left(half, low)
-            xs[u, CH : 2 * CH] = half
-            xs[u, 2 * CH : 3 * CH] = from_right(half, high)
+        up = ub[u] * mg[...]
+        if u < 3:
+            up = up * jnp.where(is_first, 0.0, 1.0)
+        elif u >= ROWS + 3:
+            up = up * jnp.where(is_last, 0.0, 1.0)
+        else:
+            recon[0, u - 3] = recon[0, u - 3] + up
+        half = up.astype(BF16)
+        xs[u, 0:CH] = from_left(half, low)
+        xs[u, CH : 2 * CH] = half
+        xs[u, 2 * CH : 3 * CH] = from_right(half, high)
 
     def window(ref, row):
         a = ref[row : row + 3]
@@ -370,14 +397,20 @@
             fs[2 * p + h, 2 * HID : 3 * HID] = from_right(x, high)
 
     def second_pair(p):
-        z = gelu(jnp.dot(w2[...], window(fs, 2 * p), preferred_element_type=F32))
-        for h in range(2):
-            x = z[:, h * W : (h + 1) * W]
-            if p == 0 and h == 0:
-                x = x * jnp.where(is_first, 0.0, 1.0)
-            if p == PAIRS and h == 1:
-                x = x * jnp.where(is_last, 0.0, 1.0)
-            gs[2 * p + h] = x.astype(BF16)
+        cuts = 2 if p in SPLIT else 1
+        size = HID // cuts
+        for n in range(cuts):
+            at = n * size
+            z = gelu(
+                jnp.dot(w2[at : at + size, :], window(fs, 2 * p), preferred_element_type=F32)
+            )
+            for h in range(2):
+                x = z[:, h * W : (h + 1) * W]
+                if p == 0 and h == 0:
+                    x = x * jnp.where(is_first, 0.0, 1.0)
+                if p == PAIRS and h == 1:
+                    x = x * jnp.where(is_last, 0.0, 1.0)
+                gs[2 * p + h, at : at + size] = x.astype(BF16)
 
     def third_pair(p):
         low, high = side_masks(F32)
@@ -388,20 +421,27 @@
                 x[CH : 2 * CH] + from_left(x[0:CH], low) + from_right(x[2 * CH : 3 * CH], high)
             )
 
-    flat_in = w_in[...].reshape(9 * CH, HID)
-    w1[...] = flat_in.T
-    for tap in range(9):
-        w2[:, tap * HID : (tap + 1) * HID] = w_mid[tap // 3, tap % 3].T
+    fetch(0).wait()
+    coarse_stage(0)
+    pl.semaphore_wait(barrier, nr - 1 + len(steps))
+    mag_send(0)
+    near_send()
+    fetch(1).wait()
+    halo_send(0)
+    for n in (5, 6, 7):
+        fetch(n).wait()
+    for level in range(1, 4):
+        halo_send(level)
+
+    for n in (2, 3, 4):
+        fetch(n).wait()
+    w1[...] = w_in[...].reshape(9 * CH, HID).T
     for dr in range(3):
         for dc in range(3):
             w3[dc * CH : (dc + 1) * CH, dr * HID : (dr + 1) * HID] = w_out[dr, dc]
-
-    coarse_stage(0)
-    pl.semaphore_wait(barrier, (nr - 1) + (ny - 1) + (nz - 1))
-    mag_send(0)
-    halo_send(0)
-    for level in range(1, 4):
-        halo_send(level)
+    for tap in range(9):
+        w2[:, tap * HID : (tap + 1) * HID] = w_mid[tap // 3, tap % 3].T
+    recon[...] = jnp.zeros_like(recon)
 
     def one_level(level, _):
         for k in range(4):
@@ -412,14 +452,31 @@
                     coarse_stage(k)
                     mag_send(k)
                 stats_stage(k)
+                if k == 3:
+                    part_r[me] = st[...]
+                    for d in range(1, nr):
+                        r_copy(d, me).start()
                 halo_wait(k)
                 spread_stage(k)
-                if k == 3:
-                    part_r[me] = tot[...]
+                near_wait()
+                if k < 3:
+                    near_send()
+                mg[...] = jnp.broadcast_to(mag_wait(k), (CH, W))
+                if k < 3:
+                    near_wait()
+                    near_send()
+                else:
                     for d in range(1, nr):
-                        r_copy(d, me).start()
-                scale_stage(k, mag_wait(k))
-
+                        r_copy(d, row_peer(d)).wait_recv()
+                    total = part_r[0]
+                    for j in range(1, nr):
+                        total = total + part_r[j]
+                    part_d[dp] = total
+                    for d in range(1, ny * nz):
+                        d_copy(d, dp).start()
+
+        for u in range(ROWS + 6):
+            scale_row(u)
         for p in range(PAIRS + 4):
             if p < PAIRS + 2:
                 first_pair(p)
@@ -427,71 +484,16 @@
                 second_pair(p - 2)
             if p >= 4:
                 third_pair(p - 4)
-            if p == 4:
-
-                @pl.when(level == 3)
-                def _():
-                    for d in range(1, nr):
-                        r_copy(d, row_peer(d)).wait_recv()
-                    tile = part_r[0]
-                    for j in range(1, nr):
-                        tile = tile + part_r[j]
-                    part_y[my_y] = tile
-                    for d in range(1, ny):
-                        y_copy(d, my_y).start()
-
-            if p == 7:
-
-                @pl.when(level == 3)
-                def _():
-                    for d in range(1, ny):
-                        y_copy(d, y_peer(d)).wait_recv()
-                    tile = part_y[0]
-                    for j in range(1, ny):
-                        tile = tile + part_y[j]
-                    part_z[my_z] = tile
-                    for d in range(1, nz):
-                        z_copy(d, my_z).start()
-
         return 0
 
     lax.fori_loop(0, 4, one_level, 0)
 
-    for d in range(1, nz):
-        z_copy(d, z_peer(d)).wait_recv()
-    tile = part_z[0]
-    for j in range(1, nz):
-        tile = tile + part_z[j]
-    lane = lanes((8, W))
-    images = ny * nz
-    group = lane // 16
-    scale = jnp.zeros((8, W), F32)
-    for level in range(4):
-        side = W // FACTORS[level]
-        scale = jnp.where(
-            group == level, 1.0 / (images * side * side * FACTORS[level]), scale
-        )
-    usage = tile * scale
-    terms = -(usage * jnp.log(usage + EPSILON))
-    square = (8, W)
-    for level in range(4):
-        mine = jnp.sum(jnp.where(group == level, terms, 0.0), axis=1, keepdims=True)
-        row = jnp.sum(
-            jnp.where(lanes(square) == subs(square), jnp.broadcast_to(mine, square), 0.0),
-            axis=0,
-            keepdims=True,
-        )
-        uent[level : level + 1, :] = row[:, 0:8]
-    entropies = jnp.sum(tile, axis=0, keepdims=True)
-    shifted = pltpu.roll(entropies, W - 64, 1)
-    lane1 = lanes((1, W))
-    scale1 = jnp.zeros((1, W), F32)
-    for level in range(4):
-        side = W // FACTORS[level]
-        scale1 = jnp.where(
-            lane1 == level, 1.0 / (images * side * side * FACTORS[level] * CH), scale1
-        )
-    sent[...] = (shifted * scale1)[:, 0:4]
+    for d in range(1, ny * nz):
+        d_copy(d, dp_peer(d)).wait_recv()
+    total = part_d[0]
+    for j in range(1, ny * nz):
+        total = total + part_d[j]
+    final[...] = total
 
     for level in range(4):
         halo_drain(level)
@@ -499,10 +501,32 @@
             mag_copy(level, d, me).wait_send()
     for d in range(1, nr):
         r_copy(d, me).wait_send()
-    for d in range(1, ny):
-        y_copy(d, my_y).wait_send()
-    for d in range(1, nz):
-        z_copy(d, my_z).wait_send()
+    for d in range(1, ny * nz):
+        d_copy(d, dp).wait_send()
+
+
+def finish(images, recon_in, sums, recon, uent, sent, sem):
+    copy = pltpu.make_async_copy(recon_in, recon, sem)
+    copy.start()
+    for level in range(4):
+        side = W // FACTORS[level]
+        usage = sums[level] * (1.0 / (images * side * side * FACTORS[level]))
+        terms = -(usage * jnp.log(usage + EPSILON))
+        shape = (W, 8)
+        group = subs(shape) // 16
+        pick = jnp.where(group == lanes(shape), 1.0, 0.0)
+        uent[level : level + 1, :] = jnp.dot(
+            terms, pick, precision=lax.Precision.HIGHEST, preferred_element_type=F32
+        )
+    lane = lanes((1, W))
+    scale = jnp.zeros((1, W), F32)
+    for level in range(4):
+        side = W // FACTORS[level]
+        scale = jnp.where(
+            lane == level, 1.0 / (images * side * side * FACTORS[level] * CH), scale
+        )
+    sent[...] = (sums[4] * scale)[:, 0:4]
+    copy.wait()
 
 
 def solution(mesh):
@@ -514,17 +538,25 @@
     vmem = pl.BlockSpec(memory_space=pltpu.VMEM)
     dma = pltpu.SemaphoreType.DMA
 
-    def on_device(*args):
-        recon, uent, sent = pl.pallas_call(
+    def on_device(lat, b1, *rest):
+        anywhere = pl.BlockSpec(memory_space=pl.ANY)
+        recon, sums = pl.pallas_call(
             functools.partial(body, ny, nz, nr),
             out_shape=(
                 jax.ShapeDtypeStruct((1, ROWS, CH, W), F32),
-                jax.ShapeDtypeStruct((4, 8), F32),
-                jax.ShapeDtypeStruct((1, 4), F32),
+                jax.ShapeDtypeStruct((5, 1, W), F32),
             ),
-            in_specs=[vmem] * 8,
-            out_specs=(vmem, vmem, vmem),
+            in_specs=[pl.BlockSpec(memory_space=pltpu.HBM)] * 8,
+            out_specs=(vmem, vmem),
             scratch_shapes=[
+                pltpu.VMEM((1, ROWS, CH, W), F32),
+                pltpu.VMEM((1, 2, 16, CH), jnp.int32),
+                pltpu.VMEM((1, 4, CH, 32), jnp.int32),
+                pltpu.VMEM((1, 8, CH, 64), jnp.int32),
+                pltpu.VMEM((1, ROWS, CH, W), jnp.int32),
+                pltpu.VMEM((3, 3, CH, HID), BF16),
+                pltpu.VMEM((3, 3, HID, HID), BF16),
+                pltpu.VMEM((3, 3, CH, HID), BF16),
                 pltpu.VMEM((HID, 9 * CH), BF16),
                 pltpu.VMEM((HID, 9 * HID), BF16),
                 pltpu.VMEM((3 * CH, 3 * HID), BF16),
@@ -535,30 +567,42 @@
                 pltpu.VMEM((ROWS, CH, W), F32),
                 pltpu.VMEM((ROWS, CH, W), F32),
                 pltpu.VMEM((ROWS, CH, W), F32),
-                pltpu.VMEM((2, HALO[0], CH, 16), jnp.int32),
+                pltpu.VMEM((2, HALO[0], 16, CH), jnp.int32),
                 pltpu.VMEM((2, HALO[1], CH, 32), jnp.int32),
                 pltpu.VMEM((2, HALO[2], CH, 64), jnp.int32),
                 pltpu.VMEM((2, HALO[3], CH, 128), jnp.int32),
                 pltpu.VMEM((4, nr, 1, W), F32),
-                pltpu.VMEM((8, W), F32),
-                pltpu.VMEM((nr, 8, W), F32),
-                pltpu.VMEM((ny, 8, W), F32),
-                pltpu.VMEM((nz, 8, W), F32),
+                pltpu.VMEM((CH, W), F32),
+                pltpu.VMEM((5, 1, W), F32),
+                pltpu.VMEM((nr, 5, 1, W), F32),
+                pltpu.VMEM((nd, 5, 1, W), F32),
+                dma((8,)),
                 dma((4, 2)),
                 dma((4, 2)),
                 dma((4, nr)),
                 dma((4, nr)),
                 dma((nr,)),
                 dma((nr,)),
-                dma((ny,)),
-                dma((ny,)),
-                dma((nz,)),
-                dma((nz,)),
+                dma((nd,)),
+                dma((nd,)),
+                pltpu.SemaphoreType.REGULAR((4,)),
             ],
             compiler_params=pltpu.CompilerParams(
-                collective_id=0, has_side_effects=True, vmem_limit_bytes=60 * 1024 * 1024
+                collective_id=0, has_side_effects=True, vmem_limit_bytes=VMEM_LIMIT
             ),
-        )(*args)
+        )(lat, jnp.swapaxes(b1, 2, 3), *rest)
+        recon, uent, sent = pl.pallas_call(
+            functools.partial(finish, nd),
+            out_shape=(
+                jax.ShapeDtypeStruct((1, ROWS, CH, W), F32),
+                jax.ShapeDtypeStruct((4, 8), F32),
+                jax.ShapeDtypeStruct((1, 4), F32),
+            ),
+            in_specs=[anywhere, vmem],
+            out_specs=(anywhere, vmem, vmem),
+            scratch_shapes=[dma],
+            compiler_params=pltpu.CompilerParams(vmem_limit_bytes=1024 * 1024),
+        )(recon, sums)
         return recon, uent, sent.reshape(4)
 
     split = P("dp", "rows", None, None)

time: 61 us -> 52.3 us (0.86)
  Pallas kernels: 54.7 us -> 49.8 us
  local copies, waits for them, and re-layouts: 5.41 us -> 1.62 us
    pallas_call x1, Pallas kernels: 54.7 us -> 48.5 us  [on_device(): pl.pallas_call(functools.partial(body, ny, nz, nr), out_shape=(jax.ShapeD...]
    unnamed x4, local copies, waits for them, and re-layouts: 5.41 us -> 1.62 us
    pallas_call x0 -> x1, Pallas kernels: none -> 1.29 us  [on_device(): pl.pallas_call(functools.partial(finish, nd), out_shape=(jax.ShapeDtypeSt...]
where the time goes in v1:
time: 52.3 us; the launch traced here: 52.1 us
  Pallas kernels  49.8 us (95%)
  local copies, waits for them, and re-layouts  1.62 us (3%)
  between operations  0.65 us (1%)
    pallas_call x1, Pallas kernels, on_device(): pl.pallas_call(functools.partial(body, ny, nz, nr), out_shape=(jax.ShapeD...  48.5 us
    unnamed x4, local copies, waits for them, and re-layouts  1.62 us
    pallas_call x1, Pallas kernels, on_device(): pl.pallas_call(functools.partial(finish, nd), out_shape=(jax.ShapeDtypeSt...  1.29 us

profile of v1, /device:TPU:1, one launch (start us, length us, event | category | flops | bytes accessed | tf_op | source)
XLA Modules:
  0.0 52.1 jit_solution(16375589999032512230)
XLA Ops:
  0.6 48.5 %shard_map.103 = (f32[1,16,32,128]{3,2,1,0:T(8,128)}, f32[5,1,128]{2,1,0:T(1,128)}) custom-call(f32[1,16,32,128]{3,2,1,0:T(8,128)} %lat_in.1, s32[1,2,16,32]{3,2,1,0:T(8,128)} %bitcast.2, s32[1,4,32,32]{3,2,1,0:T(8,128)} %b2_in.1, s32[1,8,32,64]{3,2,1,0:T(8,128)} %b3_in.1, s32[1,16,32,128]{3,2,1,0:T(8,128)} %b4_in.1, bf16[3,3,32,256]{3,2,1,0:T(8,128)(2,1)} %w_in_in.1, ...), custom_call_target="tpu_custom_call" | custom-call | tf_op jit(solution)/shard_map/pallas_call | solution.py:543
  49.2 0.0 copy-start
  49.2 0.9 %copy-done = f32[1,16,32,128]{3,2,1,0:T(8,128)S(1)} copy-done((f32[1,16,32,128]{3,2,1,0:T(8,128)S(1)}, f32[1,16,32,128]{3,2,1,0:T(8,128)}, u32[]{:S(2)}) %copy-start) | copy-done | bytes 262168
  50.1 0.0 copy-start.1
  50.1 0.7 %copy-done.1 = f32[5,1,128]{2,1,0:T(1,128)S(1)} copy-done((f32[5,1,128]{2,1,0:T(1,128)S(1)}, f32[5,1,128]{2,1,0:T(1,128)}, u32[]{:S(2)}) %copy-start.1) | copy-done | bytes 2584
  50.8 1.3 %shard_map.104 = (f32[1,16,32,128]{3,2,1,0:T(8,128)}, f32[4,8]{1,0:T(4,128)}, f32[1,4]{1,0:T(1,128)}) custom-call(f32[1,16,32,128]{3,2,1,0:T(8,128)S(1)} %copy-done, f32[5,1,128]{2,1,0:T(1,128)S(1)} %copy-done.1), custom_call_target="tpu_custom_call" | custom-call | tf_op jit(solution)/shard_map/pallas_call | solution.py:594
Async XLA Ops:
  49.2 1.0 %copy-start = (f32[1,16,32,128]{3,2,1,0:T(8,128)S(1)}, f32[1,16,32,128]{3,2,1,0:T(8,128)}, u32[]{:S(2)}) copy-start(f32[1,16,32,128]{3,2,1,0:T(8,128)} %get-tuple-element.8.recon_in) | copy-start | bytes 786436
  50.1 0.7 %copy-start.1 = (f32[5,1,128]{2,1,0:T(1,128)S(1)}, f32[5,1,128]{2,1,0:T(1,128)}, u32[]{:S(2)}) copy-start(f32[5,1,128]{2,1,0:T(1,128)} %get-tuple-element.9.sums) | copy-start | bytes 7684

commit v2 on v1

--- a/solution.py
+++ b/solution.py
@@ -14,13 +14,15 @@
 HALO = (1, 2, 2, 3)
 SHARPNESS = 2.0
 EPSILON = 1e-6
-VMEM_LIMIT = 66000000
+VMEM_LIMIT = 56545000
+PARTS = 2
 ROWS = 16
 CH = 32
 HID = 256
 W = 128
 PAIRS = ROWS // 2
-SPLIT = (0, PAIRS)
+CUTS = 2
+SPLIT = tuple(range(PAIRS + 1))
 
 
 def lanes(shape):
@@ -46,10 +48,9 @@
     return pltpu.roll(x, W - 1, 1) * high
 
 
-def gelu(x):
+def twice_gelu(x):
     inner = x * (0.7978845608028654 + (0.7978845608028654 * 0.044715) * (x * x))
-    half = 0.5 * x
-    return half + half * jnp.tanh(inner)
+    return x + x * jnp.tanh(inner)
 
 
 def block_mean(x, factor):
@@ -91,8 +92,9 @@
     w_in_in,
     w_mid_in,
     w_out_in,
+    recon_out,
+    final,
     recon,
-    final,
     lat,
     b1,
     b2,
@@ -121,6 +123,7 @@
     part_r,
     part_d,
     in_sem,
+    out_sem,
     halo_ss,
     halo_rs,
     mag_ss,
@@ -146,6 +149,13 @@
     def dp_peer(d):
         return lax.rem(my_y + d // nz, ny) * nz + lax.rem(my_z + d % nz, nz)
 
+    def away(d, n):
+        return min(d, n - d)
+
+    far_rows = sorted(range(1, nr), key=lambda d: (-away(d, nr), d))
+    far_dp = sorted(
+        range(1, ny * nz), key=lambda d: (-away(d // nz, ny) - away(d % nz, nz), d)
+    )
     steps = [] if nz == 1 else [1, nz - 1]
     steps = steps + ([] if ny == 1 else [nz, (ny - 1) * nz])
 
@@ -271,7 +281,7 @@
         mags[level, me] = row
 
     def mag_send(level):
-        for d in range(1, nr):
+        for d in far_rows:
             mag_copy(level, d, me).start()
 
     def mag_wait(level):
@@ -384,24 +394,29 @@
 
     def first_pair(p):
         low, high = side_masks(BF16)
-        z = gelu(jnp.dot(w1[...], window(xs, 2 * p), preferred_element_type=F32))
-        if p == 0:
-            z = z * jnp.where(is_first, 0.0, 1.0)
-        if p == PAIRS + 1:
-            z = z * jnp.where(is_last, 0.0, 1.0)
-        z = z.astype(BF16)
-        for h in range(2):
-            x = z[:, h * W : (h + 1) * W]
-            fs[2 * p + h, 0:HID] = from_left(x, low)
-            fs[2 * p + h, HID : 2 * HID] = x
-            fs[2 * p + h, 2 * HID : 3 * HID] = from_right(x, high)
+        size = HID // CUTS
+        for n in range(CUTS):
+            at = n * size
+            z = twice_gelu(
+                jnp.dot(w1[at : at + size, :], window(xs, 2 * p), preferred_element_type=F32)
+            )
+            if p == 0:
+                z = z * jnp.where(is_first, 0.0, 1.0)
+            if p == PAIRS + 1:
+                z = z * jnp.where(is_last, 0.0, 1.0)
+            z = z.astype(BF16)
+            for h in range(2):
+                x = z[:, h * W : (h + 1) * W]
+                fs[2 * p + h, at : at + size] = from_left(x, low)
+                fs[2 * p + h, HID + at : HID + at + size] = x
+                fs[2 * p + h, 2 * HID + at : 2 * HID + at + size] = from_right(x, high)
 
     def second_pair(p):
         cuts = 2 if p in SPLIT else 1
         size = HID // cuts
         for n in range(cuts):
             at = n * size
-            z = gelu(
+            z = twice_gelu(
                 jnp.dot(w2[at : at + size, :], window(fs, 2 * p), preferred_element_type=F32)
             )
             for h in range(2):
@@ -438,9 +453,9 @@
     w1[...] = w_in[...].reshape(9 * CH, HID).T
     for dr in range(3):
         for dc in range(3):
-            w3[dc * CH : (dc + 1) * CH, dr * HID : (dr + 1) * HID] = w_out[dr, dc]
+            w3[dc * CH : (dc + 1) * CH, dr * HID : (dr + 1) * HID] = w_out[dr, dc] * 0.5
     for tap in range(9):
-        w2[:, tap * HID : (tap + 1) * HID] = w_mid[tap // 3, tap % 3].T
+        w2[:, tap * HID : (tap + 1) * HID] = (w_mid[tap // 3, tap % 3] * 0.5).T
     recon[...] = jnp.zeros_like(recon)
 
     def one_level(level, _):
@@ -450,44 +465,62 @@
             def _(k=k):
                 if k > 0:
                     coarse_stage(k)
+                if k == 3:
+                    stats_stage(k)
+                    part_r[me] = st[...]
+                    for d in far_rows:
+                        r_copy(d, me).start()
+                if k > 0:
                     mag_send(k)
-                stats_stage(k)
-                if k == 3:
-                    part_r[me] = st[...]
-                    for d in range(1, nr):
-                        r_copy(d, me).start()
+                if k < 3:
+                    stats_stage(k)
                 halo_wait(k)
                 spread_stage(k)
-                near_wait()
-                if k < 3:
-                    near_send()
-                mg[...] = jnp.broadcast_to(mag_wait(k), (CH, W))
+                if k > 0:
+                    halo_drain(k - 1)
+                    for d in range(1, nr):
+                        mag_copy(k - 1, d, me).wait_send()
                 if k < 3:
                     near_wait()
+                if k < 2:
                     near_send()
-                else:
+                if k == 3:
                     for d in range(1, nr):
                         r_copy(d, row_peer(d)).wait_recv()
                     total = part_r[0]
                     for j in range(1, nr):
                         total = total + part_r[j]
                     part_d[dp] = total
-                    for d in range(1, ny * nz):
+                    for d in far_dp:
                         d_copy(d, dp).start()
+                mg[...] = jnp.broadcast_to(mag_wait(k), (CH, W))
+                if k < 2:
+                    near_wait()
+                    near_send()
 
         for u in range(ROWS + 6):
             scale_row(u)
-        for p in range(PAIRS + 4):
+        for p in range(PAIRS + 5):
             if p < PAIRS + 2:
                 first_pair(p)
-            if 2 <= p < PAIRS + 3:
-                second_pair(p - 2)
-            if p >= 4:
-                third_pair(p - 4)
+            if 3 <= p < PAIRS + 4:
+                second_pair(p - 3)
+            if p >= 5:
+                third_pair(p - 5)
         return 0
 
     lax.fori_loop(0, 4, one_level, 0)
 
+    copy_out = pltpu.make_async_copy(recon, recon_out, out_sem)
+    copy_out.start()
+    halo_drain(3)
+    for d in range(1, nr):
+        mag_copy(3, d, me).wait_send()
+    for d in range(1, nr):
+        r_copy(d, me).wait_send()
+    for d in range(1, ny * nz):
+        d_copy(d, dp).wait_send()
+    copy_out.wait()
     for d in range(1, ny * nz):
         d_copy(d, dp_peer(d)).wait_recv()
     total = part_d[0]
@@ -495,19 +528,22 @@
         total = total + part_d[j]
     final[...] = total
 
-    for level in range(4):
-        halo_drain(level)
-        for d in range(1, nr):
-            mag_copy(level, d, me).wait_send()
-    for d in range(1, nr):
-        r_copy(d, me).wait_send()
-    for d in range(1, ny * nz):
-        d_copy(d, dp).wait_send()
-
-
-def finish(images, recon_in, sums, recon, uent, sent, sem):
-    copy = pltpu.make_async_copy(recon_in, recon, sem)
-    copy.start()
+
+def finish(
+    images, recon_in, sums, recon, uent_out, sent_out, buf, uent, sent, in_sem, out_sem, small
+):
+    part = ROWS // PARTS
+
+    def inward(n):
+        at = pl.ds(n * part, part)
+        return pltpu.make_async_copy(recon_in.at[0, at], buf.at[at], in_sem.at[n])
+
+    def outward(n):
+        at = pl.ds(n * part, part)
+        return pltpu.make_async_copy(buf.at[at], recon.at[0, at], out_sem.at[n])
+
+    for n in range(PARTS):
+        inward(n).start()
     for level in range(4):
         side = W // FACTORS[level]
         usage = sums[level] * (1.0 / (images * side * side * FACTORS[level]))
@@ -526,7 +562,19 @@
             lane == level, 1.0 / (images * side * side * FACTORS[level] * CH), scale
         )
     sent[...] = (sums[4] * scale)[:, 0:4]
-    copy.wait()
+    pairs = (
+        pltpu.make_async_copy(uent, uent_out, small.at[0]),
+        pltpu.make_async_copy(sent, sent_out, small.at[1]),
+    )
+    for n in range(PARTS):
+        inward(n).wait()
+        outward(n).start()
+    for copy in pairs:
+        copy.start()
+    for copy in pairs:
+        copy.wait()
+    for n in range(PARTS):
+        outward(n).wait()
 
 
 def solution(mesh):
@@ -547,8 +595,9 @@
                 jax.ShapeDtypeStruct((5, 1, W), F32),
             ),
             in_specs=[pl.BlockSpec(memory_space=pltpu.HBM)] * 8,
-            out_specs=(vmem, vmem),
+            out_specs=(anywhere, vmem),
             scratch_shapes=[
+                pltpu.VMEM((1, ROWS, CH, W), F32),
                 pltpu.VMEM((1, ROWS, CH, W), F32),
                 pltpu.VMEM((1, 2, 16, CH), jnp.int32),
                 pltpu.VMEM((1, 4, CH, 32), jnp.int32),
@@ -577,6 +626,7 @@
                 pltpu.VMEM((nr, 5, 1, W), F32),
                 pltpu.VMEM((nd, 5, 1, W), F32),
                 dma((8,)),
+                dma,
                 dma((4, 2)),
                 dma((4, 2)),
                 dma((4, nr)),
@@ -599,9 +649,16 @@
                 jax.ShapeDtypeStruct((1, 4), F32),
             ),
             in_specs=[anywhere, vmem],
-            out_specs=(anywhere, vmem, vmem),
-            scratch_shapes=[dma],
-            compiler_params=pltpu.CompilerParams(vmem_limit_bytes=1024 * 1024),
+            out_specs=(anywhere, anywhere, anywhere),
+            scratch_shapes=[
+                pltpu.VMEM((ROWS, CH, W), F32),
+                pltpu.VMEM((4, 8), F32),
+                pltpu.VMEM((1, 4), F32),
+                dma((PARTS,)),
+                dma((PARTS,)),
+                dma((2,)),
+            ],
+            compiler_params=pltpu.CompilerParams(vmem_limit_bytes=VMEM_LIMIT),
         )(recon, sums)
         return recon, uent, sent.reshape(4)
 

time: 52.3 us -> 47.8 us (0.914)
  Pallas kernels: 49.8 us -> 47 us
  local copies, waits for them, and re-layouts: 1.62 us -> 0 us
    pallas_call x1, Pallas kernels: 48.5 us -> 45.3 us  [on_device(): pl.pallas_call(functools.partial(body, ny, nz, nr), out_shape=(jax.ShapeD...]
    unnamed x4 -> x0, local copies, waits for them, and re-layouts: 1.62 us -> none
where the time goes in v2:
time: 47.8 us; the launch traced here: 47.7 us
  Pallas kernels  47 us (98%)
  between operations  0.64 us (1%)
    pallas_call x1, Pallas kernels, on_device(): pl.pallas_call(functools.partial(body, ny, nz, nr), out_shape=(jax.ShapeD...  45.3 us
    pallas_call x1, Pallas kernels, on_device(): pl.pallas_call(functools.partial(finish, nd), out_shape=(jax.ShapeDtypeSt...  1.74 us

profile of v2, /device:TPU:1, one launch (start us, length us, event | category | flops | bytes accessed | tf_op | source)
XLA Modules:
  0.0 47.7 jit_solution(11612007795821585926)
XLA Ops:
  0.6 45.3 %shard_map.103 = (f32[1,16,32,128]{3,2,1,0:T(8,128)}, f32[5,1,128]{2,1,0:T(1,128)S(1)}) custom-call(f32[1,16,32,128]{3,2,1,0:T(8,128)} %lat_in.1, s32[1,2,16,32]{3,2,1,0:T(8,128)} %bitcast.2, s32[1,4,32,32]{3,2,1,0:T(8,128)} %b2_in.1, s32[1,8,32,64]{3,2,1,0:T(8,128)} %b3_in.1, s32[1,16,32,128]{3,2,1,0:T(8,128)} %b4_in.1, bf16[3,3,32,256]{3,2,1,0:T(8,128)(2,1)} %w_in_in.1, ...), custom_call_target="tpu_custom_call" | custom-call | tf_op jit(solution)/shard_map/pallas_call | solution.py:591
  45.9 1.7 %shard_map.104 = (f32[1,16,32,128]{3,2,1,0:T(8,128)}, f32[4,8]{1,0:T(4,128)}, f32[1,4]{1,0:T(1,128)}) custom-call(f32[1,16,32,128]{3,2,1,0:T(8,128)} %get-tuple-element.8.recon_in, f32[5,1,128]{2,1,0:T(1,128)S(1)} %get-tuple-element.9.sums), custom_call_target="tpu_custom_call" | custom-call | tf_op jit(solution)/shard_map/pallas_call | solution.py:644

commit v3 on v2

--- a/solution.py
+++ b/solution.py
@@ -14,8 +14,7 @@
 HALO = (1, 2, 2, 3)
 SHARPNESS = 2.0
 EPSILON = 1e-6
-VMEM_LIMIT = 56545000
-PARTS = 2
+VMEM_LIMIT = 56280000
 ROWS = 16
 CH = 32
 HID = 256
@@ -80,60 +79,59 @@
     return table.astype(BF16)
 
 
-def body(
-    ny,
-    nz,
-    nr,
-    lat_in,
-    b1_in,
-    b2_in,
-    b3_in,
-    b4_in,
-    w_in_in,
-    w_mid_in,
-    w_out_in,
-    recon_out,
-    final,
-    recon,
-    lat,
-    b1,
-    b2,
-    b3,
-    b4,
-    w_in,
-    w_mid,
-    w_out,
-    w1,
-    w2,
-    w3,
-    xs,
-    fs,
-    gs,
-    ub,
-    cs,
-    ps,
-    qs,
-    h1,
-    h2,
-    h3,
-    h4,
-    mags,
-    mg,
-    st,
-    part_r,
-    part_d,
-    in_sem,
-    out_sem,
-    halo_ss,
-    halo_rs,
-    mag_ss,
-    mag_rs,
-    pr_ss,
-    pr_rs,
-    pd_ss,
-    pd_rs,
-    near,
-):
+def body(ny, nz, nr, pieces, *refs):
+    (
+        lat_in,
+        b1_in,
+        b2_in,
+        b3_in,
+        b4_in,
+        w_in_in,
+        w_mid_in,
+        w_out_in,
+    ) = refs[:8]
+    recon_out = refs[8 : 8 + pieces]
+    (
+        final,
+        recon,
+        lat,
+        b1,
+        b2,
+        b3,
+        b4,
+        w_in,
+        w_mid,
+        w_out,
+        w1,
+        w2,
+        w3,
+        xs,
+        fs,
+        gs,
+        ub,
+        cs,
+        ps,
+        qs,
+        h1,
+        h2,
+        h3,
+        h4,
+        mags,
+        mg,
+        st,
+        part_r,
+        part_d,
+        in_sem,
+        halo_ss,
+        halo_rs,
+        mag_ss,
+        mag_rs,
+        pr_ss,
+        pr_rs,
+        pd_ss,
+        pd_rs,
+        near,
+    ) = refs[8 + pieces :]
     bits = (b1, b2, b3, b4)
     halos = (h1, h2, h3, h4)
     me = lax.axis_index("rows")
@@ -254,6 +252,13 @@
 
     def d_copy(d, slot):
         return stage_copy(part_d, pd_ss, pd_rs, d, slot, {"dp": dp_peer(d)})
+
+    def summed(ref, count):
+        parts = [ref[j] for j in range(count)]
+        while len(parts) > 1:
+            rest = [parts[-1]] if len(parts) % 2 else []
+            parts = [a + b for a, b in zip(parts[0::2], parts[1::2])] + rest
+        return parts[0]
 
     def residual_row(level, row):
         if level == 0:
@@ -289,9 +294,7 @@
             mag_copy(level, d, row_peer(d)).wait_recv()
         factor = FACTORS[level]
         side = W // factor
-        row = mags[level, 0]
-        for j in range(1, nr):
-            row = row + mags[level, j]
+        row = summed(mags.at[level], nr)
         shape = (CH, W)
         spread = jnp.where(lanes(shape) == subs(shape), jnp.broadcast_to(row, shape), 0.0)
         return jnp.sum(spread, axis=1, keepdims=True) * (1.0 / (factor * side * side))
@@ -487,10 +490,7 @@
                 if k == 3:
                     for d in range(1, nr):
                         r_copy(d, row_peer(d)).wait_recv()
-                    total = part_r[0]
-                    for j in range(1, nr):
-                        total = total + part_r[j]
-                    part_d[dp] = total
+                    part_d[dp] = summed(part_r, nr)
                     for d in far_dp:
                         d_copy(d, dp).start()
                 mg[...] = jnp.broadcast_to(mag_wait(k), (CH, W))
@@ -511,8 +511,8 @@
 
     lax.fori_loop(0, 4, one_level, 0)
 
-    copy_out = pltpu.make_async_copy(recon, recon_out, out_sem)
-    copy_out.start()
+    for n in range(ROWS):
+        recon_out[n][...] = recon[0, n]
     halo_drain(3)
     for d in range(1, nr):
         mag_copy(3, d, me).wait_send()
@@ -520,30 +520,20 @@
         r_copy(d, me).wait_send()
     for d in range(1, ny * nz):
         d_copy(d, dp).wait_send()
-    copy_out.wait()
-    for d in range(1, ny * nz):
+    for d in reversed(far_dp):
         d_copy(d, dp_peer(d)).wait_recv()
-    total = part_d[0]
-    for j in range(1, ny * nz):
-        total = total + part_d[j]
-    final[...] = total
-
-
-def finish(
-    images, recon_in, sums, recon, uent_out, sent_out, buf, uent, sent, in_sem, out_sem, small
-):
-    part = ROWS // PARTS
-
-    def inward(n):
-        at = pl.ds(n * part, part)
-        return pltpu.make_async_copy(recon_in.at[0, at], buf.at[at], in_sem.at[n])
+    final[...] = summed(part_d, ny * nz)
+
+
+def finish(images, *refs):
+    rows = refs[:ROWS]
+    sums, recon, uent_out, sent_out, uent, sent, out_sem, small = refs[ROWS:]
 
     def outward(n):
-        at = pl.ds(n * part, part)
-        return pltpu.make_async_copy(buf.at[at], recon.at[0, at], out_sem.at[n])
-
-    for n in range(PARTS):
-        inward(n).start()
+        return pltpu.make_async_copy(rows[n], recon.at[0, n], out_sem.at[n])
+
+    for n in range(ROWS):
+        outward(n).start()
     for level in range(4):
         side = W // FACTORS[level]
         usage = sums[level] * (1.0 / (images * side * side * FACTORS[level]))
@@ -566,14 +556,11 @@
         pltpu.make_async_copy(uent, uent_out, small.at[0]),
         pltpu.make_async_copy(sent, sent_out, small.at[1]),
     )
-    for n in range(PARTS):
-        inward(n).wait()
-        outward(n).start()
     for copy in pairs:
         copy.start()
     for copy in pairs:
         copy.wait()
-    for n in range(PARTS):
+    for n in range(ROWS):
         outward(n).wait()
 
 
@@ -588,14 +575,14 @@
 
     def on_device(lat, b1, *rest):
         anywhere = pl.BlockSpec(memory_space=pl.ANY)
-        recon, sums = pl.pallas_call(
-            functools.partial(body, ny, nz, nr),
+        *rows, sums = pl.pallas_call(
+            functools.partial(body, ny, nz, nr, ROWS),
             out_shape=(
-                jax.ShapeDtypeStruct((1, ROWS, CH, W), F32),
+                *(jax.ShapeDtypeStruct((CH, W), F32) for _ in range(ROWS)),
                 jax.ShapeDtypeStruct((5, 1, W), F32),
             ),
             in_specs=[pl.BlockSpec(memory_space=pltpu.HBM)] * 8,
-            out_specs=(anywhere, vmem),
+            out_specs=(vmem,) * (ROWS + 1),
             scratch_shapes=[
                 pltpu.VMEM((1, ROWS, CH, W), F32),
                 pltpu.VMEM((1, ROWS, CH, W), F32),
@@ -626,7 +613,6 @@
                 pltpu.VMEM((nr, 5, 1, W), F32),
                 pltpu.VMEM((nd, 5, 1, W), F32),
                 dma((8,)),
-                dma,
                 dma((4, 2)),
                 dma((4, 2)),
                 dma((4, nr)),
@@ -648,18 +634,16 @@
                 jax.ShapeDtypeStruct((4, 8), F32),
                 jax.ShapeDtypeStruct((1, 4), F32),
             ),
-            in_specs=[anywhere, vmem],
+            in_specs=[anywhere] * ROWS + [vmem],
             out_specs=(anywhere, anywhere, anywhere),
             scratch_shapes=[
-                pltpu.VMEM((ROWS, CH, W), F32),
                 pltpu.VMEM((4, 8), F32),
                 pltpu.VMEM((1, 4), F32),
-                dma((PARTS,)),
-                dma((PARTS,)),
+                dma((ROWS,)),
                 dma((2,)),
             ],
             compiler_params=pltpu.CompilerParams(vmem_limit_bytes=VMEM_LIMIT),
-        )(recon, sums)
+        )(*rows, sums)
         return recon, uent, sent.reshape(4)
 
     split = P("dp", "rows", None, None)

time: 47.8 us -> 46.6 us (0.975)
  Pallas kernels: 47 us -> 45.8 us
    pallas_call x1, Pallas kernels: 1.74 us -> 1.09 us  [on_device(): pl.pallas_call(functools.partial(finish, nd), out_shape=(jax.ShapeDtypeSt...]
    pallas_call x1, Pallas kernels: 45.3 us -> 44.7 us  [on_device(): pl.pallas_call(functools.partial(body, ny, nz, nr, ROWS), out_shape=(*(ja...]
where the time goes in v3:
time: 46.6 us; the launch traced here: 46.5 us
  Pallas kernels  45.8 us (98%)
  between operations  0.64 us (1%)
    pallas_call x1, Pallas kernels, on_device(): pl.pallas_call(functools.partial(body, ny, nz, nr, ROWS), out_shape=(*(ja...  44.7 us
    pallas_call x1, Pallas kernels, on_device(): pl.pallas_call(functools.partial(finish, nd), out_shape=(jax.ShapeDtypeSt...  1.09 us

profile of v3, /device:TPU:1, one launch (start us, length us, event | category | flops | bytes accessed | tf_op | source)
XLA Modules:
  0.0 46.5 jit_solution(4045356132109176064)
XLA Ops:
  0.6 44.7 %shard_map.103 = (f32[32,128]{1,0:T(8,128)S(1)}, f32[32,128]{1,0:T(8,128)S(1)}, f32[32,128]{1,0:T(8,128)S(1)}, f32[32,128]{1,0:T(8,128)S(1)}, f32[32,128]{1,0:T(...) custom-call(f32[1,16,32,128]{3,2,1,0:T(8,128)} %refs_0_.1, ...), custom_call_target="tpu_custom_call" | custom-call | tf_op jit(solution)/shard_map/pallas_call | solution.py:578
  45.4 1.1 %shard_map.104 = (f32[1,16,32,128]{3,2,1,0:T(8,128)}, f32[4,8]{1,0:T(4,128)}, f32[1,4]{1,0:T(1,128)}) custom-call(f32[32,128]{1,0:T(8,128)S(1)} %get-tuple-element.23.refs_0_, f32[32,128]{1,0:T(8,128)S(1)} %get-tuple-element.24.refs_1_, f32[32,128]{1,0:T(8,128)S(1)} %get-tuple-element.25.refs_2_, f32[32,128]{1,0:T(8,128)S(1)} %get-tuple-element.26.refs_3_, ...), custom_call_target="tpu_custom_call" | custom-call | tf_op jit(solution)/shard_map/pallas_call | solution.py:630
